TPU v7x, 32 devices: a whole 2x2x4 slice. The times are simulated.
32 devices in a mesh: seq: 4 (over z), head: 4 (over y, x), batch: 2 (over core).
Axes of the slice: x: 2, y: 2, z: 4, core: 2. Of those that a mesh axis runs over, the one named last changes fastest.
Arguments:
- tokens: bfloat16 [4096, 2560], P(('batch', 'seq'), 'head'), parts along dimension 0, may hold values from -6 to 6
- resets: int32 [4096], P(('batch', 'seq')), parts along dimension 0, may hold values 0 or 1
- w_x: bfloat16 [2560, 5120], P(None, 'head'), may hold values from -0.125 to 0.125
- w_z: bfloat16 [2560, 5120], P(None, 'head'), may hold values from -0.125 to 0.125
- w_bc: bfloat16 [2560, 256], replicated, may hold values from -0.125 to 0.125
- w_dt: bfloat16 [2560, 80], P(None, 'head'), may hold values from -0.125 to 0.125
- dt_bias: float32 [80], P('head'), may hold values from -2 to 1
- decay_rate: float32 [80], P('head'), may hold values from 0.00024414062 to 0.08
- d_skip: float32 [80], P('head'), may hold values from 0.5 to 1.5
- norm_gain: float32 [5120], P('head'), may hold values from 0.5 to 1.5
- w_out: bfloat16 [5120, 2560], P('head'), may hold values from -0.078125 to 0.078125
Outputs:
- mixed: bfloat16 [4096, 2560], P(('batch', 'seq'), 'head'), parts along dimension 0
There are 2 independent parts, one for each index of `batch`. A program takes and returns all parts, laid end to end along the dimension named above; an argument that names none is the same for every part. Nothing has to cross between parts.
All inputs are finite; a program needn't handle non-finite values. No bound on the sum of `resets` on one device may be relied on, other than what follows from the above.
Results may differ from a plain program's by a relative error of at most 0.013.
Values may be sent and summed in bfloat16 or wider, within the bound.
A program may use at most 128 MiB of HBM per device.

v0:
```python
import jax
import jax.numpy as jnp
from jax import lax
from jax.sharding import PartitionSpec as P

DI = 5120
HEADDIM = 64
NSTATE = 128
GROUP = 256


def carried_in(array, axis, combine, identity):
    count, mine = (lax.axis_size(axis), lax.axis_index(axis))
    everything = jax.tree.map(lambda part: lax.all_gather(part, axis), array)
    start = jax.tree.map(
        lambda part, zero: jnp.broadcast_to(jnp.asarray(zero, part.dtype), part.shape),
        array,
        identity,
    )

    def turn(k, before):
        reached = k < mine
        new = combine(before, jax.tree.map(lambda part: part[k], everything))
        return jax.tree.map(lambda a, b: jnp.where(reached, a, b), new, before)

    return lax.fori_loop(0, count, turn, start)


def decay_block(inputs, step_size, log_decay, in_proj, out_proj, restart, state_in):
    cumulative = jnp.cumsum(log_decay, axis=0)
    segment = jnp.cumsum(restart)
    places = jnp.arange(restart.shape[0], dtype=jnp.int32)
    same_doc = (segment[:, None] == segment[None, :]) & (places[:, None] >= places[None, :])
    scores = jnp.dot(out_proj, in_proj.T, preferred_element_type=jnp.float32)
    spread = cumulative.T[:, :, None] - cumulative.T[:, None, :]
    factor = jnp.exp(jnp.where(same_doc[None], spread, -jnp.inf))
    mixing = (factor * scores[None] * step_size.T[:, None, :]).astype(jnp.bfloat16)
    output = jnp.einsum("hts,shp->thp", mixing, inputs, preferred_element_type=jnp.float32)
    entering = jnp.where((segment == 0)[:, None], jnp.exp(cumulative), 0.0)
    carried = jnp.einsum(
        "tn,hpn->thp", out_proj.astype(jnp.float32), state_in, precision=lax.Precision.HIGHEST
    )
    output = output + entering[:, :, None] * carried
    closing = segment[-1]
    keeping = (
        jnp.where((segment == closing)[:, None], jnp.exp(cumulative[-1][None, :] - cumulative), 0.0)
        * step_size
    )
    scaled = (keeping[:, :, None] * inputs.astype(jnp.float32)).astype(jnp.bfloat16)
    update = jnp.einsum("shp,sn->hpn", scaled, in_proj, preferred_element_type=jnp.float32)
    through = jnp.where(closing == 0, jnp.exp(cumulative[-1]), 0.0)
    return (output, update + through[:, None, None] * state_in)


def on_device(tokens, resets, w_x, w_z, w_bc, w_dt, dt_bias, decay_rate, d_skip, norm_gain, w_out):
    tok_rows = tokens.shape[0]
    heads_dev = w_dt.shape[1]
    width_dev = w_x.shape[1]
    column_piece = lax.all_gather(tokens, "head", axis=1, tiled=True)
    acc_inner, acc_gate, acc_mapped, acc_step = tuple(
        (
            jnp.dot(column_piece, matrix, preferred_element_type=jnp.float32)
            for matrix in (w_x, w_z, w_bc, w_dt)
        )
    )
    inner = jax.nn.silu(acc_inner).astype(jnp.bfloat16)
    gating = acc_gate.astype(jnp.bfloat16)
    mapped = jax.nn.silu(acc_mapped).astype(jnp.bfloat16)
    step_size = jax.nn.softplus(acc_step + dt_bias)
    log_decay = -step_size * decay_rate
    blocks = tok_rows // GROUP
    out_proj = mapped[:, NSTATE:]
    sliced = (
        inner.reshape(blocks, GROUP, heads_dev, HEADDIM),
        step_size.reshape(blocks, GROUP, heads_dev),
        log_decay.reshape(blocks, GROUP, heads_dev),
        mapped[:, :NSTATE].reshape(blocks, GROUP, NSTATE),
        out_proj.reshape(blocks, GROUP, NSTATE),
        resets.reshape(blocks, GROUP),
    )

    def advance(state_in, pieces):
        output, state_out = decay_block(
            pieces[0], pieces[1], pieces[2], pieces[3], pieces[4], pieces[5], state_in
        )
        return (state_out, output)

    final_state, outputs = lax.scan(
        advance, jnp.zeros((heads_dev, HEADDIM, NSTATE), jnp.float32), sliced
    )
    cumulative = jnp.cumsum(log_decay, axis=0)
    segment = jnp.cumsum(resets)
    through = jnp.where(segment[-1] == 0, jnp.exp(cumulative[-1]), 0.0)

    def compose(earlier, latter):
        return (earlier[0] * latter[0], latter[0][:, None, None] * earlier[1] + latter[1])

    prefix = carried_in(
        (through, final_state),
        "seq",
        compose,
        (jnp.ones_like(through), jnp.zeros_like(final_state)),
    )
    incoming = prefix[1]
    entering = jnp.where((segment == 0)[:, None], jnp.exp(cumulative), 0.0)
    carried = jnp.einsum(
        "tn,hpn->thp", out_proj.astype(jnp.float32), incoming, precision=lax.Precision.HIGHEST
    )
    mixed_heads = (
        outputs.reshape(tok_rows, heads_dev, HEADDIM)
        + entering[:, :, None] * carried
        + d_skip[None, :, None] * inner.reshape(tok_rows, heads_dev, HEADDIM).astype(jnp.float32)
    )
    gated = mixed_heads.reshape(tok_rows, width_dev) * jax.nn.silu(gating.astype(jnp.float32))
    squares = lax.psum(jnp.sum(gated * gated, axis=1), "head")
    normed = (gated * lax.rsqrt(squares[:, None] / DI + 1e-05) * norm_gain).astype(jnp.bfloat16)
    partial_terms = jnp.dot(normed, w_out, preferred_element_type=jnp.float32)
    result = lax.psum_scatter(partial_terms, "head", scatter_dimension=1, tiled=True)
    return result.astype(jnp.bfloat16)


def solution(mesh):
    in_specs = (
        P(("batch", "seq"), "head"),
        P(("batch", "seq")),
        P(None, "head"),
        P(None, "head"),
        P(),
        P(None, "head"),
        P("head"),
        P("head"),
        P("head"),
        P("head"),
        P("head", None),
    )
    out_specs = P(("batch", "seq"), "head")
    return jax.shard_map(
        on_device, mesh=mesh, in_specs=in_specs, out_specs=out_specs, check_vma=False
    )
```

profile of v0, /device:TPU:24, one launch (start us, length us, event | category | flops | bytes accessed | tf_op | source)
XLA Modules:
  0.0 316.8 jit_solution(1247841689320259402)
XLA Ops:
  6.5 0.7 all-gather.5.cloned.1.call-update
  7.3 0.7 reshape.208
  8.0 41.7 %all-gather.5.cloned.1.call-done = bf16[512,2560]{1,0:T(8,128)(2,1)} async-done(((bf16[512,640]{1,0:T(8,128)(2,1)}), bf16[512,2560]{1,0:T(8,128)(2,1)}) %all-gather.5.cloned.1.call-update) | async-done | bytes 2621456 | tf_op jit(solution)/shard_map/all_gather | solution.py:59
  49.7 2.7 multiply_convert_fusion.8
  52.5 1.4 compare_select_fusion.1
  54.0 0.6 reshape.209
  54.6 0.6 reshape.210
  55.2 7.4 %multiply_convert_fusion.6 = bf16[512,1280]{1,0:T(8,128)(2,1)S(1)} fusion(bf16[512,2560]{1,0:T(8,128)(2,1)} %all-gather.5.cloned.1.call-done, bf16[2560,1280]{1,0:T(8,128)(2,1)} %param.17), kind=kOutput, calls=%fused_computation.68 | convolution fusion | flops 3358720000 | bytes 10485760 | tf_op jit(solution)/shard_map/dot_general | solution.py:62
  62.7 1.2 copy-done.2
  63.8 1.5 copy.48
  65.3 3.2 reshape.211
  68.5 1.3 copy.51
  69.8 81.0 %while.27 = (s32[]{:T(128)}, f32[20,64,128]{2,1,0:T(8,128)S(1)}, f32[2,256,20,64]{1,0,3,2:T(2,128)}, s32[2,256]{1,0:T(2,128)S(1)}, f32[2,256,20]{1,0,2:T(2,128)}...) while((s32[]{:T(128)}, f32[20,64,128]{2,1,0:T(8,128)S(1)}, ...), condition=%wide.region_5.6_spmd.clone, body=%wide.region_0.5_spmd.clone.sunk | while | flops 781505152 | bytes 14305162 | solution.py:88
  69.8 0.8 constant_dynamic-slice_fusion.6
  70.7 0.6 reduce-window.56
  71.6 0.6 copy.82
  72.2 0.3 reduce-window.54
  72.9 0.2 fusion.84
  73.2 2.7 fusion.86
  75.9 0.6 slice.92
  76.6 0.7 broadcast_compare_fusion.6
  77.3 0.2 slice_reduce_fusion.10
  77.5 0.7 exponential_select_fusion.3
  78.2 1.5 fusion.87
  79.6 1.3 copy.84
  81.0 27.0 %dynamic_update_slice.6 = f32[2,256,20,64]{1,0,3,2:T(2,128)} dynamic-update-slice(f32[2,256,20,64]{1,0,3,2:T(2,128)} %get-tuple-element.389, f32[1,256,20,64]{1,0,3,2:T(1,128)S(1)} %copy.84, s32[]{:T(128)} %get-tuple-element.387, s32[]{:T(128)} %constant.77.clone.1..sunk, s32[]{:T(128)} %constant.77.clone.1..sunk, s32[]{:T(128)} %constant.77.clone.1..sunk) | dynamic-update-slice | bytes 2621444 | tf_op jit(solution)/shard_map/while/body/jit(dynamic_update_index_in_dim)/dynamic_update_slice | solution.py:88
  108.7 1.5 convolution_add_fusion.3
  110.3 0.8 constant_dynamic-slice_fusion.6
  111.2 0.6 reduce-window.56
  112.1 0.6 copy.82
  112.7 0.3 reduce-window.54
  113.4 0.2 fusion.84
  113.6 2.8 fusion.86
  116.4 0.6 slice.92
  117.1 0.7 broadcast_compare_fusion.6
  117.8 0.2 slice_reduce_fusion.10
  118.0 0.7 exponential_select_fusion.3
  118.7 1.5 fusion.87
  120.1 1.3 copy.84
  121.5 27.0 %dynamic_update_slice.6 = f32[2,256,20,64]{1,0,3,2:T(2,128)} dynamic-update-slice(f32[2,256,20,64]{1,0,3,2:T(2,128)} %get-tuple-element.389, f32[1,256,20,64]{1,0,3,2:T(1,128)S(1)} %copy.84, s32[]{:T(128)} %get-tuple-element.387, s32[]{:T(128)} %constant.77.clone.1..sunk, s32[]{:T(128)} %constant.77.clone.1..sunk, s32[]{:T(128)} %constant.77.clone.1..sunk) | dynamic-update-slice | bytes 2621444 | tf_op jit(solution)/shard_map/while/body/jit(dynamic_update_index_in_dim)/dynamic_update_slice | solution.py:88
  149.2 1.5 convolution_add_fusion.3
  150.8 0.8 copy-done.1
  151.6 0.2 reduce-scatter.2.cloned.1.call-start
  151.9 0.3 reduce-window.34
  152.5 0.6 slice.51
  153.6 2.9 copy.55
  156.6 1.2 reduce-window.38
  157.8 0.2 slice_reduce_fusion.3
  158.1 4.8 %reshape.214 = f32[512,20,64]{0,2,1:T(8,128)} reshape(f32[2,256,20,64]{1,0,3,2:T(2,128)} %get-tuple-element.147) | data formatting | bytes 5242880 | tf_op jit(solution)/shard_map/reshape | solution.py:110
  163.0 0.2 fusion.52
  163.1 7.5 %all-gather.1 = f32[4,1,20]{2,1,0:T(1,128)S(1)} all-gather(f32[1,1,20]{2,1,0:T(1,128)S(1)} %bitcast.161), channel_id=1, replica_groups=mesh['seq'=4,'head'=4,'batch'=2] {'seq'}, dimensions={0}, use_global_device_ids=true | all-gather | bytes 400 | tf_op jit(solution)/shard_map/all_gather | solution.py:14
  170.7 33.4 %all-gather.7.cloned.1.call-done = f32[80,64,128]{2,1,0:T(8,128)} async-done(((f32[20,64,128]{2,1,0:T(8,128)}), f32[80,64,128]{2,1,0:T(8,128)}) %all-gather.7.cloned.1.call-update) | async-done | bytes 2621456 | tf_op jit(solution)/shard_map/all_gather | solution.py:14
  204.1 5.1 %while.28 = (s32[]{:T(128)}, f32[20,64,128]{2,1,0:T(8,128)S(1)}, s32[]{:T(128)}, f32[4,20]{1,0:T(4,128)S(1)}, f32[4,20,64,128]{3,2,1,0:T(8,128)}, /*index=5*/s32[]{:T(128)}, s32[]{:T(128)}) while((s32[]{:T(128)}, f32[20,64,128]{2,1,0:T(8,128)S(1)}, s32[]{:T(128)}, f32[4,20]{1,0:T(4,128)S(1)}, f32[4,20,64,128]{3,2,1,0:T(8,128)}, ...), condition=%wide.region_11.12_spmd.clone, body=%wide.region_10.11_spmd.clone.sunk | while | flops 655364 | bytes 1966425 | solution.py:26
  204.1 1.3 fusion.88
  205.4 1.2 fusion.88
  206.7 1.2 fusion.88
  207.9 1.2 fusion.88
  209.2 5.5 %multiply_add_fusion = f32[512,20,64]{0,2,1:T(8,128)} fusion(f32[512,20,64]{0,2,1:T(8,128)} %bitcast.144, f32[512,20,64]{0,2,1:T(8,128)} %reshape.214, f32[20,64,128]{2,1,0:T(8,128)S(1)} %get-tuple-element.149, f32[20]{0:T(128)S(1)} %copy-done.13, f32[512,20]{0,1:T(8,128)S(1)} %exponential_select_fusion.1, bf16[512,256]{1,0:T(8,128)(2,1)S(1)} %copy-done.8), kind=kOutput, calls=%fused_computation.67 | convolution fusion | flops 1009254400 | bytes 8700416 | tf_op jit(solution)/shard_map/tn,hpn->thp/dot_general | solution.py:106
  214.7 3.2 %copy.56 = f32[512,1280]{1,0:T(8,128)} copy(f32[512,1280]{0,1:T(8,128)} %bitcast.145) | data formatting | bytes 5242880 | tf_op jit(solution)/shard_map/reshape | solution.py:114
  218.0 9.7 %multiply_reduce_fusion = (f32[512]{0:T(512)S(1)}, f32[512,1280]{1,0:T(8,128)}) fusion(f32[512,1280]{1,0:T(8,128)} %copy.56, bf16[512,2560]{1,0:T(8,128)(2,1)} %all-gather.5.cloned.1.call-done, bf16[2560,1280]{1,0:T(8,128)(2,1)} %param.18), kind=kOutput, calls=%fused_computation.66 | convolution fusion | flops 3361340928 | bytes 14419968 | tf_op jit(solution)/shard_map/dot_general | solution.py:62
  227.7 10.0 %psum.7 = f32[512]{0:T(512)S(1)} all-reduce(f32[512]{0:T(512)S(1)} %get-tuple-element.275), channel_id=1, replica_groups=mesh['seq'=4,'head'=4,'batch'=2] {'head'}, use_global_device_ids=true, to_apply=%region_13.14 | all-reduce | flops 512 | bytes 4096 | tf_op jit(solution)/shard_map/psum | solution.py:115
  237.7 9.6 %fusion.41 = f32[512,2560]{1,0:T(8,128)} fusion(bf16[1280,2560]{1,0:T(8,128)(2,1)} %param.25, f32[512,1280]{1,0:T(8,128)} %get-tuple-element.276, f32[1280]{0:T(1024)S(1)} %copy-done.15, f32[512]{0:T(512)S(1)} %add_rsqrt_fusion), kind=kOutput, calls=%fused_computation.69 | convolution fusion | flops 3357409280 | bytes 14425088 | tf_op jit(solution)/shard_map/dot_general | solution.py:117
  247.4 60.7 %reduce-scatter.2.cloned.1.call-done = f32[512,640]{1,0:T(8,128)} async-done(((f32[512,2560]{1,0:T(8,128)}), f32[512,640]{1,0:T(8,128)}) %reduce-scatter.2.cloned.1.call-update) | async-done | bytes 1310736 | tf_op jit(solution)/shard_map/reduce_scatter | solution.py:118
  308.0 2.2 convert_element_type.46
  (97 shorter events, 2.3 us)
Async XLA Ops:
  6.5 43.2 %copy-start = (bf16[2560,256]{1,0:T(8,128)(2,1)S(1)}, bf16[2560,256]{1,0:T(8,128)(2,1)}, u32[]{:S(2)}) copy-start(bf16[2560,256]{1,0:T(8,128)(2,1)} %param.19) | copy-start | bytes 3932164
  6.5 43.2 %all-gather.5.cloned.1.call-start = ((), (), s32[]{:S(2)}) async-start(), calls=%async_computation.1 | async-start | bytes 3276800 | tf_op jit(solution)/shard_map/all_gather | solution.py:59
  7.3 196.8 %all-gather.7.cloned.1.call-start = ((), (), s32[]{:S(2)}) async-start(), calls=%async_computation.3 | async-start | bytes 3276800 | tf_op jit(solution)/shard_map/all_gather | solution.py:14
  8.0 44.5 %copy-start.10 = (bf16[2560,20]{0,1:T(8,128)(2,1)S(1)}, bf16[2560,20]{0,1:T(8,128)(2,1)}, u32[]{:S(2)}) copy-start(bf16[2560,20]{0,1:T(8,128)(2,1)} %param.20) | copy-start | bytes 307204
  8.0 44.5 %copy-start.12 = (f32[20]{0:T(128)S(1)}, f32[20]{0:T(128)}, u32[]{:S(2)}) copy-start(f32[20]{0:T(128)} %param.22) | copy-start | bytes 244
  8.0 44.5 %copy-start.14 = (f32[20]{0:T(128)S(1)}, f32[20]{0:T(128)}, u32[]{:S(2)}) copy-start(f32[20]{0:T(128)} %param.21) | copy-start | bytes 244
  49.7 2.8 copy-start.6
  52.5 1.5 copy-start.7
  62.7 1.2 copy-start.2
  69.8 82.1 %copy-start.11 = (s32[512]{0:T(512)S(1)}, s32[512]{0:T(512)}, u32[]{:S(2)}) copy-start(s32[512]{0:T(512)} %param.16) | copy-start | bytes 6148
  70.6 2.5 copy-start.3
  73.2 4.1 %copy-start.5 = (f32[3,8,2,128]{3,1,2,0:T(8,128)S(1)}, f32[3,8,2,128]{3,1,2,0:T(8,128)}, u32[]{:S(2)}) copy-start(f32[3,8,2,128]{3,1,2,0:T(8,128)} %copy.82) | copy-start | bytes 73732 | tf_op jit(solution)/shard_map/while
  73.2 4.3 %copy-start.4 = (f32[1,256,20]{1,0,2:T(1,128)S(1)}, f32[1,256,20]{1,0,2:T(1,128)}, u32[]{:S(2)}) copy-start(f32[1,256,20]{1,0,2:T(1,128)} %copy-done.3) | copy-start | bytes 61444 | tf_op jit(solution)/shard_map/while
  111.1 2.5 copy-start.3
  113.6 4.1 %copy-start.5 = (f32[3,8,2,128]{3,1,2,0:T(8,128)S(1)}, f32[3,8,2,128]{3,1,2,0:T(8,128)}, u32[]{:S(2)}) copy-start(f32[3,8,2,128]{3,1,2,0:T(8,128)} %copy.82) | copy-start | bytes 73732 | tf_op jit(solution)/shard_map/while
  113.6 4.3 %copy-start.4 = (f32[1,256,20]{1,0,2:T(1,128)S(1)}, f32[1,256,20]{1,0,2:T(1,128)}, u32[]{:S(2)}) copy-start(f32[1,256,20]{1,0,2:T(1,128)} %copy-done.3) | copy-start | bytes 61444 | tf_op jit(solution)/shard_map/while
  150.8 0.8 copy-start.1
  150.8 5.8 %copy-start.9 = (f32[512,20]{0,1:T(8,128)S(1)}, f32[512,20]{0,1:T(8,128)}, u32[]{:S(2)}) copy-start(f32[512,20]{0,1:T(8,128)} %get-tuple-element.274) | copy-start | bytes 122884
  151.6 156.4 %reduce-scatter.2.cloned.1.call-start = ((), (), s32[]{:S(2)}) async-start(), calls=%async_computation.2 | async-start | bytes 6553600 | tf_op jit(solution)/shard_map/reduce_scatter | solution.py:118
  204.1 5.1 %copy-start.8 = (bf16[512,256]{1,0:T(8,128)(2,1)S(1)}, bf16[512,256]{1,0:T(8,128)(2,1)}, u32[]{:S(2)}) copy-start(bf16[512,256]{1,0:T(8,128)(2,1)} %copy-done.7) | copy-start | bytes 786436
  204.1 5.1 %copy-start.13 = (f32[20]{0:T(128)S(1)}, f32[20]{0:T(128)}, u32[]{:S(2)}) copy-start(f32[20]{0:T(128)} %param.23) | copy-start | bytes 244
  218.0 19.8 %copy-start.15 = (f32[1280]{0:T(1024)S(1)}, f32[1280]{0:T(1024)}, u32[]{:S(2)}) copy-start(f32[1280]{0:T(1024)} %param.24) | copy-start | bytes 15364
Sparse Core Ops, SparseCore 0:
  9.2 40.4 all-gather.4
  151.7 52.2 all-gather.6
  247.5 60.5 reduce-scatter.1
where the time goes:
time: 323 us; the launch traced here: 317 us
  waiting for transfers between devices  136 us (42%)
  local copies, waits for them, and re-layouts  84.1 us (26%)
  matrix products  48.3 us (15%)
  blocking collectives  17.6 us (5%)
  other arithmetic  14.4 us (4%)
  between operations  13.9 us (4%)
    reduce_scatter x1, waiting for transfers between devices, on_device(): lax.psum_scatter(partial_terms, 'head', scatter_dimension=1, tiled=True)  60.7 us
    dynamic_update_slice x4, local copies, waits for them, and re-layouts, on_device(): lax.scan(advance, jnp.zeros((heads_dev, HEADDIM, NSTATE), jnp.float32), s...  56.8 us
    all_gather x1, waiting for transfers between devices, on_device(): column_piece = lax.all_gather(tokens, 'head', axis=1, tiled=True)  41.7 us
    all_gather x1, waiting for transfers between devices, carried_in(): everything = jax.tree.map(lambda part: lax.all_gather(part, axis), array)  33.4 us
    dot_general x4, matrix products, on_device(): jnp.dot(column_piece, matrix, preferred_element_type=jnp.float32)  21.3 us
    psum x1, blocking collectives, on_device(): squares = lax.psum(jnp.sum(gated * gated, axis=1), 'head')  10 us
    dot_general x1, matrix products, on_device(): partial_terms = jnp.dot(normed, w_out, preferred_element_type=jnp.float32)  9.59 us
    all_gather x1, blocking collectives, carried_in(): everything = jax.tree.map(lambda part: lax.all_gather(part, axis), array)  7.55 us
  transfers between devices with their start and end apart: 3, of which 3 were waited for; matrix products, arithmetic and copies ran while one was open for 4% of the time, Pallas kernels for 0%

commit v1 on v0

v1 whole, which is shorter than its diff:
```python
import functools

import jax
import jax.numpy as jnp
from jax import lax
from jax.experimental import pallas as pl
from jax.experimental.pallas import tpu as pltpu
from jax.sharding import PartitionSpec as P

HEADDIM = 64
NSTATE = 128
GROUP = 256
LANES = 128
F32 = jnp.float32
BF16 = jnp.bfloat16
MESH = pl.DeviceIdType.MESH
VMEM = pl.BlockSpec(memory_space=pltpu.VMEM)
SMEM = pl.BlockSpec(memory_space=pltpu.SMEM)
ANY = pl.BlockSpec(memory_space=pl.ANY)
EPS = 1e-05


def peers():
    me = lax.axis_index("head")
    across = me + 1 - 2 * lax.rem(me, 2)
    along = lax.rem(me + 2, 4)
    corner = lax.rem(across + 2, 4)
    return me, across, along, corner


def greet(axis, others):
    barrier = pltpu.get_barrier_semaphore()
    for other in others:
        pl.semaphore_signal(barrier, inc=1, device_id={axis: other}, device_id_type=MESH)
    pl.semaphore_wait(barrier, len(others))


def remote(axis, to, src, dst, send, recv):
    return pltpu.make_async_remote_copy(
        src_ref=src, dst_ref=dst, send_sem=send, recv_sem=recv, device_id={axis: to}, device_id_type=MESH
    )


def silu(v):
    return v / (1.0 + jnp.exp(-v))


def project_kernel(
    tok, w_x, w_z, w_bc, w_dt, bias, inner, gating, mapped, step,
    got, vx, vz, acc_x, acc_z, acc_m, acc_s, load, send, recv,
):
    me, across, along, corner = peers()
    rows, depth = tok.shape
    half = rows // 2
    lo, hi = pl.ds(0, half), pl.ds(half, half)
    loads = []
    owners = (me, across, along, corner)
    for k, owner in enumerate(owners):
        span = pl.ds(pl.multiple_of(owner * depth, LANES), depth)
        loads.append((
            pltpu.make_async_copy(w_x.at[span], vx.at[k], load.at[2 * k]),
            pltpu.make_async_copy(w_z.at[span], vz.at[k], load.at[2 * k + 1]),
        ))
    for pair in loads:
        for copy in pair:
            copy.start()
    greet("head", (across, along))
    copies = [
        remote("head", across, tok.at[lo], got.at[0, lo], send.at[0], recv.at[0]),
        remote("head", along, tok.at[hi], got.at[1, hi], send.at[1], recv.at[1]),
        remote("head", across, tok.at[hi], got.at[0, hi], send.at[2], recv.at[2]),
        remote("head", along, tok.at[lo], got.at[1, lo], send.at[3], recv.at[3]),
        remote("head", along, got.at[0, lo], got.at[2, lo], send.at[4], recv.at[4]),
        remote("head", across, got.at[1, hi], got.at[2, hi], send.at[5], recv.at[5]),
    ]
    for copy in copies[:4]:
        copy.start()

    wide = 256
    tiles = vx.shape[2] // wide

    def accumulate(k, block):
        for copy in loads[k]:
            copy.wait()
        span = pl.ds(pl.multiple_of(owners[k] * depth, LANES), depth)
        last = k == 3

        def tile(i, _):
            cols = pl.ds(pl.multiple_of(i * wide, wide), wide)
            a = jnp.dot(block[...], vx[k, :, cols], preferred_element_type=F32)
            b = jnp.dot(block[...], vz[k, :, cols], preferred_element_type=F32)
            if k:
                a, b = a + acc_x[:, cols], b + acc_z[:, cols]
            if last:
                inner[:, cols] = silu(a).astype(BF16)
                gating[:, cols] = b.astype(BF16)
            else:
                acc_x[:, cols] = a
                acc_z[:, cols] = b
            return 0

        lax.fori_loop(0, tiles, tile, 0)
        m = jnp.dot(block[...], w_bc[span, :], preferred_element_type=F32)
        s = jnp.dot(block[...], w_dt[span, :], preferred_element_type=F32)
        if k:
            m, s = m + acc_m[...], s + acc_s[...]
        if last:
            mapped[...] = silu(m).astype(BF16)
            v = s + bias[...]
            step[...] = jnp.zeros_like(step)
            step[:, : v.shape[1]] = jnp.maximum(v, 0.0) + jnp.log1p(jnp.exp(-jnp.abs(v)))
        else:
            acc_m[...] = m
            acc_s[...] = s

    accumulate(0, tok)
    copies[0].wait_recv()
    copies[4].start()
    copies[1].wait_recv()
    copies[5].start()
    copies[2].wait_recv()
    accumulate(1, got.at[0])
    copies[3].wait_recv()
    accumulate(2, got.at[1])
    copies[4].wait_recv()
    copies[5].wait_recv()
    accumulate(3, got.at[2])
    for copy in copies:
        copy.wait_send()


def project(tokens, w_x, w_z, w_bc, w_dt, dt_bias):
    rows, depth = tokens.shape
    width, heads, both = w_x.shape[1], w_dt.shape[1], w_bc.shape[1]
    padded = -(-heads // LANES) * LANES
    sds = jax.ShapeDtypeStruct
    return pl.pallas_call(
        project_kernel,
        out_shape=(
            sds((rows, width), BF16), sds((rows, width), BF16),
            sds((rows, both), BF16), sds((rows, padded), F32),
        ),
        in_specs=[VMEM, ANY, ANY, VMEM, VMEM, VMEM],
        out_specs=(VMEM,) * 4,
        scratch_shapes=[
            pltpu.VMEM((3, rows, depth), BF16),
            pltpu.VMEM((4, depth, width), BF16),
            pltpu.VMEM((4, depth, width), BF16),
            pltpu.VMEM((rows, width), F32),
            pltpu.VMEM((rows, width), F32),
            pltpu.VMEM((rows, both), F32),
            pltpu.VMEM((rows, heads), F32),
            pltpu.SemaphoreType.DMA((8,)),
            pltpu.SemaphoreType.DMA((6,)),
            pltpu.SemaphoreType.DMA((6,)),
        ],
        compiler_params=pltpu.CompilerParams(
            collective_id=0, has_side_effects=True, vmem_limit_bytes=60 * 1024 * 1024
        ),
    )(tokens, w_x, w_z, w_bc, w_dt, dt_bias.reshape(1, heads))


def scan_kernel(
    chain, heads, inner, gating, mapped, step, resets, rate, skip, gain, out, squares,
    cum, cumt, stept, keep, enter, score, local, first, thr, arrived, leaving, y, send, recv,
):
    me = lax.axis_index("seq")
    rows, width = inner.shape
    blocks = rows // GROUP
    pairs = width // LANES
    per = LANES // HEADDIM
    chunk = leaving.shape[2]
    chunks = width // chunk
    upper, lower = lax.rem(me + 1, chain), lax.rem(me + chain - 1, chain)
    greet("seq", (upper, lower))

    ti = lax.broadcasted_iota(jnp.int32, (GROUP, GROUP), 0)
    si = lax.broadcasted_iota(jnp.int32, (GROUP, GROUP), 1)
    causal = ti >= si
    tri = jnp.where(causal, 1.0, 0.0).astype(F32)
    lane = lax.broadcasted_iota(jnp.int32, (GROUP, LANES), 1)

    def column(ref, b, h):
        return jnp.sum(jnp.where(lane == h, ref[b], 0.0), axis=1, keepdims=True)

    def spread(ref, b, j):
        return jnp.where(lane < HEADDIM, column(ref, b, per * j), column(ref, b, per * j + 1))

    for b in range(blocks):
        span = pl.ds(b * GROUP, GROUP)
        stp = step[span, :]
        decay = -stp * rate[...]
        total = jnp.dot(tri, decay, preferred_element_type=F32, precision=lax.Precision.HIGHEST)
        cum[b] = total
        cumt[b] = total.T
        stept[b] = stp.T
        starts = resets[:, b * GROUP : (b + 1) * GROUP].astype(F32)
        seg_c = jnp.sum(tri * starts, axis=1, keepdims=True)
        start_c = jnp.sum(jnp.where(ti == si, jnp.broadcast_to(starts, (GROUP, GROUP)), 0.0), axis=1, keepdims=True)
        seg_r = jnp.sum(jnp.where(ti <= si, jnp.broadcast_to(start_c, (GROUP, GROUP)), 0.0), axis=0, keepdims=True)
        seg_end = seg_c[GROUP - 1 :, :]
        last = total[GROUP - 1 :, :]
        keep[b] = jnp.where(seg_c == seg_end, jnp.exp(last - total), 0.0) * stp
        enter[b] = jnp.where(seg_c == 0.0, jnp.exp(total), 0.0)
        bm, cm = mapped[span, :NSTATE], mapped[span, NSTATE:]
        dots = lax.dot_general(cm, bm, (((1,), (1,)), ((), ())), preferred_element_type=F32)
        score[b] = jnp.where(causal & (seg_c == seg_r), dots, 0.0)

    turned = [mapped[b * GROUP : (b + 1) * GROUP, :NSTATE].astype(F32).T.astype(BF16) for b in range(blocks)]

    def states(j, _):
        cols = pl.ds(pl.multiple_of(j * LANES, LANES), LANES)
        state = None
        for b in range(blocks):
            span = pl.ds(b * GROUP, GROUP)
            scaled = (spread(keep, b, j) * inner[span, cols].astype(F32)).astype(BF16)
            new = jnp.dot(turned[b], scaled, preferred_element_type=F32)
            through = spread(enter, b, j)[GROUP - 1 :, :]
            thr[b, :, cols] = through
            first[b, :, cols] = jnp.zeros((NSTATE, LANES), F32) if state is None else state
            state = new if state is None else through * state + new
        local[:, cols] = state
        return 0

    lax.fori_loop(0, pairs, states, 0)

    def down(c):
        return remote("seq", upper, leaving.at[c], arrived.at[c], send.at[c], recv.at[c])

    def combine(c, seen):
        cols = pl.ds(pl.multiple_of(c * chunk, chunk), chunk)
        value = local[:, cols]
        if seen:
            factor = thr[0, :, cols]
            for b in range(1, blocks):
                factor = factor * thr[b, :, cols]
            value = value + factor * arrived[c].astype(F32)
        leaving[c] = value.astype(BF16)
        down(c).start()

    @pl.when(me == 0)
    def _():
        arrived[...] = jnp.zeros_like(arrived)

        def turn(c, _):
            combine(c, False)
            return 0

        lax.fori_loop(0, chunks, turn, 0)

    offset = jnp.minimum(3 * me - 2, pairs - chunks)

    def within(j, _):
        cols = pl.ds(pl.multiple_of(j * LANES, LANES), LANES)
        for b in range(blocks):
            span = pl.ds(b * GROUP, GROUP)
            x = inner[span, cols]
            parts = []
            for k in range(per):
                h = per * j + k
                gap = column(cum, b, h) - cumt[b, pl.ds(h, 1), :]
                mixing = (jnp.exp(jnp.minimum(gap, 0.0)) * score[b] * stept[b, pl.ds(h, 1), :]).astype(BF16)
                parts.append(jnp.dot(mixing, x, preferred_element_type=F32))
            value = jnp.where(lane < HEADDIM, parts[0], parts[1])
            d = jnp.where(lane < HEADDIM, skip[per * j], skip[per * j + 1])
            y[span, cols] = value + d * x.astype(F32)
        c = j - offset

        @pl.when((me > 0) & (c >= 0) & (c < chunks))
        def _():
            down(c).wait_recv()

            @pl.when(me < chain - 1)
            def _():
                combine(c, True)

        return 0

    lax.fori_loop(0, pairs, within, 0)

    def finish(j, sums):
        cols = pl.ds(pl.multiple_of(j * LANES, LANES), LANES)
        tiles = chunk // LANES
        incoming = arrived[j // tiles, :, pl.ds(pl.multiple_of(lax.rem(j, tiles) * LANES, LANES), LANES)].astype(F32)
        new = []
        for b in range(blocks):
            span = pl.ds(b * GROUP, GROUP)
            state = first[b, :, cols] + incoming
            carried = jnp.dot(mapped[span, NSTATE:], state.astype(BF16), preferred_element_type=F32)
            value = y[span, cols] + spread(enter, b, j) * carried
            gated = value * silu(gating[span, cols].astype(F32))
            out[span, cols] = (gated * gain[:, cols]).astype(BF16)
            new.append(sums[b] + gated * gated)
            incoming = thr[b, :, cols] * incoming
        return tuple(new)

    sums = lax.fori_loop(0, pairs, finish, tuple(jnp.zeros((GROUP, LANES), F32) for _ in range(blocks)))
    for b in range(blocks):
        squares[:, b * GROUP : (b + 1) * GROUP] = lax.dot_general(
            jnp.ones((8, LANES), F32), sums[b], (((1,), (1,)), ((), ())),
            preferred_element_type=F32, precision=lax.Precision.HIGHEST,
        )

    @pl.when(me < chain - 1)
    def _():
        for c in range(chunks):
            down(c).wait_send()


def scan(chain, heads, inner, gating, mapped, step, resets, decay_rate, d_skip, norm_gain):
    rows, width = inner.shape
    blocks, padded = rows // GROUP, step.shape[1]
    chunk = 2 * LANES
    chunks = width // chunk
    sds = jax.ShapeDtypeStruct
    rate = jnp.pad(decay_rate.reshape(1, heads), ((0, 0), (0, padded - heads)))
    return pl.pallas_call(
        functools.partial(scan_kernel, chain, heads),
        out_shape=(sds((rows, width), BF16), sds((8, rows), F32)),
        in_specs=[VMEM] * 6 + [SMEM, VMEM],
        out_specs=(VMEM, VMEM),
        scratch_shapes=[
            pltpu.VMEM((blocks, GROUP, padded), F32),
            pltpu.VMEM((blocks, padded, GROUP), F32),
            pltpu.VMEM((blocks, padded, GROUP), F32),
            pltpu.VMEM((blocks, GROUP, padded), F32),
            pltpu.VMEM((blocks, GROUP, padded), F32),
            pltpu.VMEM((blocks, GROUP, GROUP), F32),
            pltpu.VMEM((NSTATE, width), F32),
            pltpu.VMEM((blocks, NSTATE, width), F32),
            pltpu.VMEM((blocks, 1, width), F32),
            pltpu.VMEM((chunks, NSTATE, chunk), BF16),
            pltpu.VMEM((chunks, NSTATE, chunk), BF16),
            pltpu.VMEM((rows, width), F32),
            pltpu.SemaphoreType.DMA((chunks,)),
            pltpu.SemaphoreType.DMA((chunks,)),
        ],
        compiler_params=pltpu.CompilerParams(
            collective_id=1, has_side_effects=True, vmem_limit_bytes=60 * 1024 * 1024
        ),
    )(inner, gating, mapped, step, resets.reshape(1, rows), rate, d_skip, norm_gain.reshape(1, width))


def output_kernel(total, g, squares, w, out, vw, others, sent, got, load, send, recv, sq_send, sq_recv):
    me, across, along, corner = peers()
    rows = g.shape[0]
    half = rows // 2
    width = out.shape[1]
    lo, hi = pl.ds(0, half), pl.ds(half, half)
    order = (corner, across, along, me)
    loads = [
        pltpu.make_async_copy(
            w.at[:, pl.ds(pl.multiple_of(owner * width, LANES), width)], vw.at[k], load.at[k]
        )
        for k, owner in enumerate(order)
    ]
    for copy in loads:
        copy.start()
    greet("head", (across, along, corner))
    small = [
        remote("head", to, squares, others.at[k], sq_send.at[k], sq_recv.at[k])
        for k, to in enumerate((across, along, corner))
    ]
    for copy in small:
        copy.start()

    def share(k, span):
        return jnp.dot(g[span, :], vw[k], preferred_element_type=F32)

    copies = [
        remote("head", to, sent.at[k], got.at[k], send.at[k], recv.at[k])
        for k, to in enumerate((across, along, across, along, along, across))
    ]

    def put(k, value):
        sent[k] = value.astype(BF16)
        copies[k].start()

    loads[0].wait()
    put(0, share(0, lo))
    put(1, share(0, hi))
    loads[1].wait()
    put(2, share(1, lo))
    loads[2].wait()
    put(3, share(2, hi))
    value = share(2, lo)
    copies[0].wait_recv()
    put(4, value + got[0].astype(F32))
    value = share(1, hi)
    copies[1].wait_recv()
    put(5, value + got[1].astype(F32))
    loads[3].wait()
    for copy in small:
        copy.wait_recv()
    squared = squares[...] + others[0] + others[1] + others[2]
    scale = lax.rsqrt(squared / total + EPS)
    scale = jnp.broadcast_to(scale[:1, :], (LANES, rows)).T
    for span, base, pick in ((lo, 0, (2, 4)), (hi, half, (3, 5))):
        value = share(3, span)
        for k in pick:
            copies[k].wait_recv()
            value = value + got[k].astype(F32)
        factor = scale[base : base + half, :]
        for i in range(width // LANES):
            cols = slice(i * LANES, (i + 1) * LANES)
            out[span, cols] = (value[:, cols] * factor).astype(BF16)
    for copy in copies + small:
        copy.wait_send()


def output(total, g, squares, w_out, width):
    rows, depth = g.shape
    half = rows // 2
    return pl.pallas_call(
        functools.partial(output_kernel, total),
        out_shape=jax.ShapeDtypeStruct((rows, width), BF16),
        in_specs=[VMEM, VMEM, ANY],
        out_specs=VMEM,
        scratch_shapes=[
            pltpu.VMEM((4, depth, width), BF16),
            pltpu.VMEM((3, 8, rows), F32),
            pltpu.VMEM((6, half, width), BF16),
            pltpu.VMEM((6, half, width), BF16),
            pltpu.SemaphoreType.DMA((4,)),
            pltpu.SemaphoreType.DMA((6,)),
            pltpu.SemaphoreType.DMA((6,)),
            pltpu.SemaphoreType.DMA((3,)),
            pltpu.SemaphoreType.DMA((3,)),
        ],
        compiler_params=pltpu.CompilerParams(
            collective_id=2, has_side_effects=True, vmem_limit_bytes=60 * 1024 * 1024
        ),
    )(g, squares, w_out)


def solution(mesh):
    chain, split = mesh.shape["seq"], mesh.shape["head"]

    def on_device(tokens, resets, w_x, w_z, w_bc, w_dt, dt_bias, decay_rate, d_skip, norm_gain, w_out):
        inner, gating, mapped, step = project(tokens, w_x, w_z, w_bc, w_dt, dt_bias)
        g, squares = scan(
            chain, w_dt.shape[1], inner, gating, mapped, step, resets, decay_rate, d_skip, norm_gain
        )
        return output(float(w_x.shape[1] * split), g, squares, w_out, tokens.shape[1])

    in_specs = (
        P(("batch", "seq"), "head"),
        P(("batch", "seq")),
        P(None, "head"),
        P(None, "head"),
        P(),
        P(None, "head"),
        P("head"),
        P("head"),
        P("head"),
        P("head"),
        P("head", None),
    )
    return jax.shard_map(
        on_device, mesh=mesh, in_specs=in_specs, out_specs=P(("batch", "seq"), "head"), check_vma=False
    )
```

time: 323 us -> 90 us (0.28); the launches traced: 317 us -> 89.7 us
  waiting for transfers between devices: 136 us -> 0 us
  Pallas kernels: 0 us -> 83.2 us
  local copies, waits for them, and re-layouts: 84.1 us -> 6.49 us
  matrix products: 48.3 us -> 0 us
  blocking collectives: 17.6 us -> 0 us
  other arithmetic: 14.4 us -> 0 us
  between operations: 13.9 us -> 0.03 us
    pallas_call x0 -> x3, Pallas kernels: none -> 83.2 us  [the longest x1 32.8 us: project(): pl.pallas_call(project_kernel, out_shape=(sds((rows, width), BF16), sds((...]
    all_gather x2 -> x0, waiting for transfers between devices: 75 us -> none  [the longest x1 41.7 us: on_device(): column_piece = lax.all_gather(tokens, 'head', axis=1, tiled=True)]
    reduce_scatter x1 -> x0, waiting for transfers between devices: 60.7 us -> none  [on_device(): lax.psum_scatter(partial_terms, 'head', scatter_dimension=1, tiled=True)]
    dynamic_update_slice x4 -> x0, local copies, waits for them, and re-layouts: 56.8 us -> none  [on_device(): lax.scan(advance, jnp.zeros((heads_dev, HEADDIM, NSTATE), jnp.float32), s...]
    dot_general x14 -> x0, matrix products: 48.3 us -> none  [the longest x4 21.3 us: on_device(): jnp.dot(column_piece, matrix, preferred_element_type=jnp.float32)]
    reshape x6 -> x1, local copies, waits for them, and re-layouts: 13.2 us -> 1.29 us  [scan(): norm_gain.reshape(1, width)]
    psum x1 -> x0, blocking collectives: 10 us -> none  [on_device(): squares = lax.psum(jnp.sum(gated * gated, axis=1), 'head')]
    all_gather x1 -> x0, blocking collectives: 7.55 us -> none  [carried_in(): everything = jax.tree.map(lambda part: lax.all_gather(part, axis), array)]
  transfers between devices with their start and end apart: 3 -> 0, of which waited for: 3 -> 0; matrix products, arithmetic and copies ran while one was open for 4% -> 0% of each run, Pallas kernels for 0% -> 0%
where the time goes in v1:
time: 90 us; the launch traced here: 89.7 us
  Pallas kernels  83.2 us (92%)
  local copies, waits for them, and re-layouts  6.49 us (7%)
    pallas_call x1, Pallas kernels, project(): pl.pallas_call(project_kernel, out_shape=(sds((rows, width), BF16), sds((...  32.8 us
    pallas_call x1, Pallas kernels, scan(): pl.pallas_call(functools.partial(scan_kernel, chain, heads), out_shape=(s...  25.6 us
    pallas_call x1, Pallas kernels, output(): pl.pallas_call(functools.partial(output_kernel, total), out_shape=jax.Sha...  24.9 us
    unnamed x2, local copies, waits for them, and re-layouts  4.01 us

profile of v1, /device:TPU:24, one launch (start us, length us, event | category | flops | bytes accessed | tf_op | source)
XLA Modules:
  0.0 89.7 jit_solution(16015935016954264181)
XLA Ops:
  0.0 1.2 %pad.4.rate = f32[1,128]{1,0:T(1,128)} pad(f32[1,20]{1,0:T(1,128)} %bitcast.5, f32[]{:T(128)} %constant.2.clone.1), padding=0_0x0_108 | pad | bytes 596 | tf_op jit(solution)/shard_map/jit(_pad)/pad | solution.py:316
  1.2 1.3 %reshape.15.gain = f32[1,1280]{1,0:T(1,128)} reshape(f32[1280]{0:T(1024)} %param.20) | data formatting | bytes 10240 | tf_op jit(solution)/shard_map/reshape | solution.py:341
  2.5 2.0 %copy.12.w_dt = bf16[2560,20]{1,0:T(8,128)(2,1)} copy(bf16[2560,20]{0,1:T(8,128)(2,1)} %param.16) | data formatting | bytes 204800 | tf_op args[5]
  4.5 32.8 %shard_map.109 = (bf16[512,1280]{1,0:T(8,128)(2,1)}, bf16[512,1280]{1,0:T(8,128)(2,1)}, bf16[512,256]{1,0:T(8,128)(2,1)}, f32[512,128]{1,0:T(8,128)}) custom-call(bf16[512,640]{1,0:T(8,128)(2,1)} %tok.1, bf16[2560,1280]{1,0:T(8,128)(2,1)} %w_x.1, bf16[2560,1280]{1,0:T(8,128)(2,1)} %w_z.1, bf16[2560,256]{1,0:T(8,128)(2,1)} %w_bc.1, ...), custom_call_target="tpu_custom_call" | custom-call | tf_op jit(solution)/shard_map/pallas_call | solution.py:137
  37.3 25.6 %shard_map.110 = (bf16[512,1280]{1,0:T(8,128)(2,1)}, f32[8,512]{1,0:T(8,128)}) custom-call(bf16[512,1280]{1,0:T(8,128)(2,1)} %get-tuple-element.11.inner, bf16[512,1280]{1,0:T(8,128)(2,1)} %get-tuple-element.12.gating, bf16[512,256]{1,0:T(8,128)(2,1)} %get-tuple-element.13.mapped, f32[512,128]{1,0:T(8,128)} %get-tuple-element.14.step, s32[1,512]{1,0:T(1,128)} %bitcast.3, ...), custom_call_target="tpu_custom_call" | custom-call | tf_op jit(solution)/shard_map/pallas_call | solution.py:317
  62.9 24.9 %shard_map.111 = bf16[512,640]{1,0:T(8,128)(2,1)} custom-call(bf16[512,1280]{1,0:T(8,128)(2,1)} %get-tuple-element.15.g, f32[8,512]{1,0:T(8,128)} %get-tuple-element.16.squares, bf16[1280,2560]{1,0:T(8,128)(2,1)} %w.1), custom_call_target="tpu_custom_call" | custom-call | tf_op jit(solution)/shard_map/pallas_call | solution.py:414
  87.7 2.0 %copy.14 = bf16[512,640]{1,0:T(8,128)(2,1)} copy(bf16[512,640]{1,0:T(8,128)(2,1)} %shard_map.111) | data formatting | bytes 1310720

commit v2 on v0

v2 whole, which is shorter than its diff:
```python
import functools

import jax
import jax.numpy as jnp
from jax import lax
from jax.experimental import pallas as pl
from jax.experimental.pallas import tpu as pltpu
from jax.sharding import PartitionSpec as P

HEADDIM = 64
NSTATE = 128
GROUP = 256
LANES = 128
F32 = jnp.float32
BF16 = jnp.bfloat16
MESH = pl.DeviceIdType.MESH
VMEM = pl.BlockSpec(memory_space=pltpu.VMEM)
SMEM = pl.BlockSpec(memory_space=pltpu.SMEM)
ANY = pl.BlockSpec(memory_space=pl.ANY)
EPS = 1e-05


def peers():
    me = lax.axis_index("head")
    across = me + 1 - 2 * lax.rem(me, 2)
    along = lax.rem(me + 2, 4)
    corner = lax.rem(across + 2, 4)
    return me, across, along, corner


def remote(axis, to, src, dst, send, recv):
    return pltpu.make_async_remote_copy(
        src_ref=src, dst_ref=dst, send_sem=send, recv_sem=recv, device_id={axis: to}, device_id_type=MESH
    )


def silu(v):
    return v / (1.0 + jnp.exp(-v))


class Scratch:
    def __init__(self, names, refs):
        for name, ref in zip(names, refs):
            setattr(self, name, ref)


def dot(a, b):
    return jnp.dot(a, b, preferred_element_type=F32)


def dot_nt(a, b, precision=None):
    return lax.dot_general(a, b, (((1,), (1,)), ((), ())), preferred_element_type=F32, precision=precision)


def kernel(chain, total, names, tok, resets, w_x, w_z, w_bc, w_dt, bias, rate, skip, gain, w_out, out, *refs):
    r = Scratch(names, refs)
    me, across, along, corner = peers()
    pos = lax.axis_index("seq")
    upper, lower = lax.rem(pos + 1, chain), lax.rem(pos + chain - 1, chain)
    rows, depth = tok.shape
    width = w_x.shape[1]
    heads = w_dt.shape[0]
    blocks, pairs, per = rows // GROUP, width // LANES, LANES // HEADDIM
    half = GROUP // 2
    owners = (me, across, along, corner)

    def span_of(owner):
        return pl.ds(pl.multiple_of(owner * depth, LANES), depth)

    def rows_of(b):
        return pl.ds(b * GROUP, GROUP)

    def cols_of(j):
        return pl.ds(pl.multiple_of(j * LANES, LANES), LANES)

    loads = [
        (
            pltpu.make_async_copy(w_x.at[span_of(owner)], r.vx.at[k], r.load.at[3 * k]),
            pltpu.make_async_copy(w_z.at[span_of(owner)], r.vz.at[k], r.load.at[3 * k + 1]),
            pltpu.make_async_copy(w_bc.at[span_of(owner)], r.vb.at[k], r.load.at[3 * k + 2]),
        )
        for k, owner in enumerate(owners)
    ]
    order = (corner, across, along, me)
    out_loads = [
        pltpu.make_async_copy(w_out.at[:, span_of(owner)], r.vw.at[k], r.load_out.at[k])
        for k, owner in enumerate(order)
    ]
    for k in (0, 1):
        for copy in loads[k]:
            copy.start()

    barrier = pltpu.get_barrier_semaphore()
    for other in (across, along, corner):
        pl.semaphore_signal(barrier, inc=1, device_id={"head": other}, device_id_type=MESH)
    for other in (upper, lower):
        pl.semaphore_signal(barrier, inc=1, device_id={"seq": other}, device_id_type=MESH)
    pl.semaphore_wait(barrier, 5)

    gathers = []
    for b in range(blocks):
        lo, hi = pl.ds(b * GROUP, half), pl.ds(b * GROUP + half, half)
        plan = (
            (across, tok.at[lo], r.got.at[0, lo]),
            (along, tok.at[hi], r.got.at[1, hi]),
            (across, tok.at[hi], r.got.at[0, hi]),
            (along, tok.at[lo], r.got.at[1, lo]),
            (along, r.got.at[0, lo], r.got.at[2, lo]),
            (across, r.got.at[1, hi], r.got.at[2, hi]),
        )
        gathers.append([
            remote("head", to, src, dst, r.g_send.at[6 * b + i], r.g_recv.at[6 * b + i])
            for i, (to, src, dst) in enumerate(plan)
        ])
    for copy in gathers[0][:4]:
        copy.start()

    wide = 256

    def accumulate(b, k):
        if b == 0:
            for copy in loads[k]:
                copy.wait()
            if k == 0:
                for later in (2, 3):
                    for copy in loads[later]:
                        copy.start()
            if k == 3:
                for copy in out_loads:
                    copy.start()
        rs = rows_of(b)
        block = tok if k == 0 else r.got.at[k - 1]

        def tile(i, _):
            cols = pl.ds(pl.multiple_of(i * wide, wide), wide)
            x = block[rs, :]
            v, z = dot(x, r.vx[k, :, cols]), dot(x, r.vz[k, :, cols])
            if k:
                v, z = v + r.acc_x[:, cols], z + r.acc_z[:, cols]
            if k == 3:
                r.inner[rs, cols] = silu(v).astype(BF16)
                r.gating[rs, cols] = z.astype(BF16)
            else:
                r.acc_x[:, cols] = v
                r.acc_z[:, cols] = z
            return 0

        lax.fori_loop(0, width // wide, tile, 0)
        m = dot(block[rs, :], r.vb[k])
        s = dot_nt(block[rs, :], w_dt[:, span_of(owners[k])])
        if k:
            m, s = m + r.acc_m[...], s + r.acc_s[...]
        if k == 3:
            r.mapped[rs, :] = silu(m).astype(BF16)
            v = s + bias[...]
            r.step[...] = jnp.zeros_like(r.step)
            r.step[:, :heads] = jnp.maximum(v, 0.0) + jnp.log1p(jnp.exp(-jnp.abs(v)))
        else:
            r.acc_m[...] = m
            r.acc_s[...] = s

    def relay(b):
        gathers[b][0].wait_recv()
        gathers[b][4].start()
        gathers[b][1].wait_recv()
        gathers[b][5].start()
        if b + 1 < blocks:
            for copy in gathers[b + 1][:4]:
                copy.start()

    def project(b):
        gathers[b][2].wait_recv()
        accumulate(b, 1)
        gathers[b][3].wait_recv()
        accumulate(b, 2)
        gathers[b][4].wait_recv()
        gathers[b][5].wait_recv()
        accumulate(b, 3)

    ti = lax.broadcasted_iota(jnp.int32, (GROUP, GROUP), 0)
    si = lax.broadcasted_iota(jnp.int32, (GROUP, GROUP), 1)
    causal = ti >= si
    tri = jnp.where(causal, 1.0, 0.0).astype(F32)
    lane = lax.broadcasted_iota(jnp.int32, (GROUP, LANES), 1)
    r.rate[...] = jnp.zeros_like(r.rate)
    r.rate[:, :heads] = rate[...]

    def column(ref, b, h):
        return jnp.sum(jnp.where(lane == h, ref[b], 0.0), axis=1, keepdims=True)

    def spread(ref, b, j):
        return jnp.where(lane < HEADDIM, column(ref, b, per * j), column(ref, b, per * j + 1))

    def prepare(b):
        rs = rows_of(b)
        stp = r.step[...]
        decay = -stp * r.rate[...]
        cum = jnp.dot(tri, decay, preferred_element_type=F32, precision=lax.Precision.HIGHEST)
        r.cum[b] = cum
        r.cumt[b] = cum.T
        r.stept[b] = stp.T
        starts = resets[:, b * GROUP : (b + 1) * GROUP].astype(F32)
        whole = jnp.broadcast_to(starts, (GROUP, GROUP))
        seg_c = jnp.sum(tri * starts, axis=1, keepdims=True)
        start_c = jnp.sum(jnp.where(ti == si, whole, 0.0), axis=1, keepdims=True)
        seg_r = jnp.sum(jnp.where(ti <= si, jnp.broadcast_to(start_c, (GROUP, GROUP)), 0.0), axis=0, keepdims=True)
        last = cum[GROUP - 1 :, :]
        r.keep[b] = jnp.where(seg_c == seg_c[GROUP - 1 :, :], jnp.exp(last - cum), 0.0) * stp
        r.enter[b] = jnp.where(seg_c == 0.0, jnp.exp(cum), 0.0)
        dots = dot_nt(r.mapped[rs, NSTATE:], r.mapped[rs, :NSTATE])
        r.score[b] = jnp.where(causal & (seg_c == seg_r), dots, 0.0)

    def states(b):
        rs = rows_of(b)
        turned = r.mapped[rs, :NSTATE].astype(F32).T.astype(BF16)

        def turn(j, _):
            cols = cols_of(j)
            scaled = (spread(r.keep, b, j) * r.inner[rs, cols].astype(F32)).astype(BF16)
            new = dot(turned, scaled)
            through = spread(r.enter, b, j)[GROUP - 1 :, :]
            r.thr[b, :, cols] = through
            if b:
                new = new + through * r.state[b - 1, :, cols]
            r.state[b, :, cols] = new
            if b == blocks - 1:

                @pl.when(pos == 0)
                def _():
                    combine(j, False)

            return 0

        lax.fori_loop(0, pairs, turn, 0)

    def down(c):
        return remote("seq", upper, r.leaving.at[c], r.arrived.at[c], r.c_send.at[c], r.c_recv.at[c])

    def combine(c, seen):
        cols = cols_of(c)
        value = r.state[blocks - 1, :, cols]
        if seen:
            factor = r.thr[0, :, cols]
            for b in range(1, blocks):
                factor = factor * r.thr[b, :, cols]
            value = value + factor * r.arrived[c].astype(F32)
        r.leaving[c] = value.astype(BF16)
        down(c).start()

    def receive(c):
        down(c).wait_recv()

        @pl.when(pos < chain - 1)
        def _():
            combine(c, True)

    early = pairs // 2

    def within(b):
        rs = rows_of(b)

        def turn(j, _):
            cols = cols_of(j)
            x = r.inner[rs, cols]
            parts = []
            for k in range(per):
                h = per * j + k
                gap = column(r.cum, b, h) - r.cumt[b, pl.ds(h, 1), :]
                weight = jnp.exp(jnp.minimum(gap, 0.0)) * r.score[b] * r.stept[b, pl.ds(h, 1), :]
                parts.append(dot(weight.astype(BF16), x))
            d = jnp.where(lane < HEADDIM, skip[per * j], skip[per * j + 1])
            r.y[rs, cols] = jnp.where(lane < HEADDIM, parts[0], parts[1]) + d * x.astype(F32)
            if b == blocks - 1:

                @pl.when((pos == 1) & (j >= early))
                def _():
                    receive(j - early)

            return 0

        lax.fori_loop(0, pairs, turn, 0)

    @pl.when(pos == 0)
    def _():
        r.arrived[...] = jnp.zeros_like(r.arrived)

    accumulate(0, 0)
    relay(0)
    project(0)
    prepare(0)
    states(0)
    for b in range(1, blocks):
        relay(b)
        within(b - 1)
        accumulate(b, 0)
        project(b)
        prepare(b)
        states(b)
    within(blocks - 1)

    r.sums[...] = jnp.zeros_like(r.sums)

    def finish(j, _):
        @pl.when((pos > 1) | ((pos == 1) & (j >= pairs - early)))
        def _():
            receive(j)

        cols = cols_of(j)
        incoming = r.arrived[j].astype(F32)
        for b in range(blocks):
            rs = rows_of(b)
            state = incoming + r.state[b - 1, :, cols] if b else incoming
            carried = dot(r.mapped[rs, NSTATE:], state.astype(BF16))
            value = r.y[rs, cols] + spread(r.enter, b, j) * carried
            gated = value * silu(r.gating[rs, cols].astype(F32))
            r.g[rs, cols] = (gated * gain[pl.ds(j, 1), :]).astype(BF16)
            r.sums[rs, :] = r.sums[rs, :] + gated * gated
            incoming = r.thr[b, :, cols] * incoming
        return 0

    lax.fori_loop(0, pairs, finish, 0)

    for copy in out_loads:
        copy.wait()
    small = [
        remote("head", to, r.squares, r.others.at[k], r.q_send.at[k], r.q_recv.at[k])
        for k, to in enumerate((across, along, corner))
    ]
    scatters = [
        [
            remote("head", to, r.sent.at[6 * b + k], r.back.at[6 * b + k], r.o_send.at[6 * b + k], r.o_recv.at[6 * b + k])
            for k, to in enumerate((across, along, across, along, along, across))
        ]
        for b in range(blocks)
    ]

    def put(b, k, value):
        r.sent[6 * b + k] = value.astype(BF16)
        scatters[b][k].start()

    def share(k, rs):
        return dot(r.g[rs, :], r.vw[k])

    def direct(b):
        lo, hi = pl.ds(b * GROUP, half), pl.ds(b * GROUP + half, half)
        put(b, 0, share(0, lo))
        put(b, 1, share(0, hi))
        put(b, 2, share(1, lo))
        put(b, 3, share(2, hi))

    def joined(b):
        lo, hi = pl.ds(b * GROUP, half), pl.ds(b * GROUP + half, half)
        value = share(2, lo)
        scatters[b][0].wait_recv()
        put(b, 4, value + r.back[6 * b].astype(F32))
        value = share(1, hi)
        scatters[b][1].wait_recv()
        put(b, 5, value + r.back[6 * b + 1].astype(F32))

    for b in range(blocks):
        direct(b)
        if b == 0:
            r.squares[...] = dot_nt(jnp.ones((8, LANES), F32), r.sums[...], lax.Precision.HIGHEST)
            for copy in small:
                copy.start()
        if b:
            joined(b - 1)
    joined(blocks - 1)
    own = r.y
    for b in range(blocks):
        own[rows_of(b), :depth] = share(3, rows_of(b))
    for copy in small:
        copy.wait_recv()
    squared = r.squares[...] + r.others[0] + r.others[1] + r.others[2]
    scale = lax.rsqrt(squared / total + EPS)
    r.sums[...] = jnp.broadcast_to(scale[:1, :], (LANES, rows)).T
    for b in range(blocks):
        for base, picks in ((b * GROUP, (2, 4)), (b * GROUP + half, (3, 5))):
            span = pl.ds(base, half)
            for k in picks:
                scatters[b][k].wait_recv()
            for i in range(depth // LANES):
                cols = slice(i * LANES, (i + 1) * LANES)
                value = own[span, cols]
                for k in picks:
                    value = value + r.back[6 * b + k, :, cols].astype(F32)
                out[span, cols] = (value * r.sums[span, :]).astype(BF16)

    for group in gathers + scatters + [small]:
        for copy in group:
            copy.wait_send()

    @pl.when(pos < chain - 1)
    def _():
        for c in range(pairs):
            down(c).wait_send()


def layer(chain, split, tokens, resets, w_x, w_z, w_bc, w_dt, dt_bias, decay_rate, d_skip, norm_gain, w_out):
    rows, depth = tokens.shape
    width, heads, both = w_x.shape[1], w_dt.shape[1], w_bc.shape[1]
    padded = -(-heads // LANES) * LANES
    blocks, pairs = rows // GROUP, width // LANES
    half = GROUP // 2
    vm, dma = pltpu.VMEM, pltpu.SemaphoreType.DMA
    scratch = dict(
        got=vm((3, rows, depth), BF16),
        vx=vm((4, depth, width), BF16),
        vz=vm((4, depth, width), BF16),
        vb=vm((4, depth, both), BF16),
        vw=vm((4, width, depth), BF16),
        acc_x=vm((GROUP, width), F32),
        acc_z=vm((GROUP, width), F32),
        acc_m=vm((GROUP, both), F32),
        acc_s=vm((GROUP, heads), F32),
        inner=vm((rows, width), BF16),
        gating=vm((rows, width), BF16),
        mapped=vm((rows, both), BF16),
        step=vm((GROUP, padded), F32),
        rate=vm((1, padded), F32),
        cum=vm((blocks, GROUP, padded), F32),
        cumt=vm((blocks, padded, GROUP), F32),
        stept=vm((blocks, padded, GROUP), F32),
        keep=vm((blocks, GROUP, padded), F32),
        enter=vm((blocks, GROUP, padded), F32),
        score=vm((blocks, GROUP, GROUP), F32),
        state=vm((blocks, NSTATE, width), F32),
        thr=vm((blocks, 1, width), F32),
        arrived=vm((pairs, NSTATE, LANES), BF16),
        leaving=vm((pairs, NSTATE, LANES), BF16),
        y=vm((rows, width), F32),
        g=vm((rows, width), BF16),
        sums=vm((rows, LANES), F32),
        squares=vm((8, rows), F32),
        others=vm((3, 8, rows), F32),
        sent=vm((6 * blocks, half, depth), BF16),
        back=vm((6 * blocks, half, depth), BF16),
        load=dma((12,)),
        load_out=dma((4,)),
        g_send=dma((6 * blocks,)),
        g_recv=dma((6 * blocks,)),
        c_send=dma((pairs,)),
        c_recv=dma((pairs,)),
        o_send=dma((6 * blocks,)),
        o_recv=dma((6 * blocks,)),
        q_send=dma((3,)),
        q_recv=dma((3,)),
    )
    return pl.pallas_call(
        functools.partial(kernel, chain, float(width * split), tuple(scratch)),
        out_shape=jax.ShapeDtypeStruct((rows, depth), BF16),
        in_specs=[VMEM, VMEM, ANY, ANY, ANY, VMEM, VMEM, VMEM, SMEM, VMEM, ANY],
        out_specs=VMEM,
        scratch_shapes=list(scratch.values()),
        compiler_params=pltpu.CompilerParams(
            collective_id=0, has_side_effects=True, vmem_limit_bytes=60 * 1024 * 1024
        ),
    )(
        tokens, resets.reshape(1, rows), w_x, w_z, w_bc, w_dt.T, dt_bias.reshape(1, heads),
        decay_rate.reshape(1, heads), d_skip, norm_gain.reshape(pairs, LANES), w_out,
    )


def solution(mesh):
    in_specs = (
        P(("batch", "seq"), "head"),
        P(("batch", "seq")),
        P(None, "head"),
        P(None, "head"),
        P(),
        P(None, "head"),
        P("head"),
        P("head"),
        P("head"),
        P("head"),
        P("head", None),
    )
    return jax.shard_map(
        functools.partial(layer, mesh.shape["seq"], mesh.shape["head"]),
        mesh=mesh,
        in_specs=in_specs,
        out_specs=P(("batch", "seq"), "head"),
        check_vma=False,
    )
```

time: 323 us -> 77.7 us (0.24); the launches traced: 317 us -> 77.6 us
  waiting for transfers between devices: 136 us -> 0 us
  local copies, waits for them, and re-layouts: 84.1 us -> 1.98 us
  Pallas kernels: 0 us -> 75.6 us
  matrix products: 48.3 us -> 0 us
  blocking collectives: 17.6 us -> 0 us
  other arithmetic: 14.4 us -> 0 us
  between operations: 13.9 us -> 0.01 us
    pallas_call x0 -> x1, Pallas kernels: none -> 75.6 us  [layer(): pl.pallas_call(functools.partial(kernel, chain, float(width * split), tup...]
    all_gather x2 -> x0, waiting for transfers between devices: 75 us -> none  [the longest x1 41.7 us: on_device(): column_piece = lax.all_gather(tokens, 'head', axis=1, tiled=True)]
    reduce_scatter x1 -> x0, waiting for transfers between devices: 60.7 us -> none  [on_device(): lax.psum_scatter(partial_terms, 'head', scatter_dimension=1, tiled=True)]
    dynamic_update_slice x4 -> x0, local copies, waits for them, and re-layouts: 56.8 us -> none  [on_device(): lax.scan(advance, jnp.zeros((heads_dev, HEADDIM, NSTATE), jnp.float32), s...]
    dot_general x14 -> x0, matrix products: 48.3 us -> none  [the longest x4 21.3 us: on_device(): jnp.dot(column_piece, matrix, preferred_element_type=jnp.float32)]
    reshape x6 -> x0, local copies, waits for them, and re-layouts: 13.2 us -> none  [the longest x1 4.82 us: on_device(): outputs.reshape(tok_rows, heads_dev, HEADDIM)]
    psum x1 -> x0, blocking collectives: 10 us -> none  [on_device(): squares = lax.psum(jnp.sum(gated * gated, axis=1), 'head')]
    all_gather x1 -> x0, blocking collectives: 7.55 us -> none  [carried_in(): everything = jax.tree.map(lambda part: lax.all_gather(part, axis), array)]
  transfers between devices with their start and end apart: 3 -> 0, of which waited for: 3 -> 0; matrix products, arithmetic and copies ran while one was open for 4% -> 0% of each run, Pallas kernels for 0% -> 0%
where the time goes in v2:
time: 77.7 us; the launch traced here: 77.6 us
  Pallas kernels  75.6 us (97%)
  local copies, waits for them, and re-layouts  1.98 us (3%)
    pallas_call x1, Pallas kernels, layer(): pl.pallas_call(functools.partial(kernel, chain, float(width * split), tup...  75.6 us
    unnamed x1, local copies, waits for them, and re-layouts  1.98 us

profile of v2, /device:TPU:24, one launch (start us, length us, event | category | flops | bytes accessed | tf_op | source)
XLA Modules:
  0.0 77.6 jit_solution(2082091666327897509)
XLA Ops:
  0.0 75.6 %shard_map.109 = bf16[512,640]{1,0:T(8,128)(2,1)} custom-call(bf16[512,640]{1,0:T(8,128)(2,1)} %tok.1, s32[1,512]{1,0:T(1,128)} %bitcast.7, bf16[2560,1280]{1,0:T(8,128)(2,1)} %w_x.1, bf16[2560,1280]{1,0:T(8,128)(2,1)} %w_z.1, bf16[2560,256]{1,0:T(8,128)(2,1)} %w_bc.1, bf16[20,2560]{1,0:T(8,128)(2,1)} %bitcast.5, f32[1,20]{1,0:T(1,128)} %bitcast.8, ...), custom_call_target="tpu_custom_call" | custom-call | tf_op jit(solution)/shard_map/pallas_call | solution.py:449
  75.6 2.0 %copy.13 = bf16[512,640]{1,0:T(8,128)(2,1)} copy(bf16[512,640]{1,0:T(8,128)(2,1)} %shard_map.109) | data formatting | bytes 1310720
